TPU v7x, 32 devices: a whole 2x2x4 slice. The times are simulated.
32 devices in a mesh: group: 2 (over x), tile: 16 (over z, y, core).
Axes of the slice: x: 2, y: 2, z: 4, core: 2. Of those that a mesh axis runs over, the one named last changes fastest.
Arguments:
- hadamard: int32 [128, 1152], P(None, 'tile'), may hold values from -1 to 1, as said below
- stroke: float32 [2304], P(('group', 'tile')), parts along dimension 0, may hold values from 0.3 to 1
- influence: bfloat16 [3, 2304, 8192], P(None, ('group', 'tile')), parts along dimension 1, may hold values from -0.4375 to 0.4375
- amplitude: float32 [1024, 16, 16], P(('group', 'tile')), parts along dimension 0, may hold values from 0.3 to 1
- aberration: float32 [1024, 16, 16], P(('group', 'tile')), parts along dimension 0, may hold values from -3 to 3
- valid_mask: int32 [1024], P(('group', 'tile')), parts along dimension 0, may hold values from 0 to 1, as said below
Outputs:
- imat: float32 [2304, 2, 512], P(('group', 'tile')), parts along dimension 0
There are 2 independent parts, one for each index of `group`. A program takes and returns all parts, laid end to end along the dimension named above; an argument that names none is the same for every part. Nothing has to cross between parts.
Inputs may be any that keep to these rules, and one draw needn't show every extreme that they name: `hadamard`: each column is one column of a Sylvester-Hadamard matrix whose order is the least power of two not below 1152, restricted to 128 distinct rows of it; different actuators take different columns. `valid_mask`: every pupil tile of 32 subapertures holds at least one valid subaperture.
All inputs are finite; a program needn't handle non-finite values.
Results may differ from a plain program's by a relative error of at most 0.0055.
Values may be sent and summed in bfloat16 or wider, within the bound.
A program may use at most 128 MiB of HBM per device.

v0:
```python
import functools
import math

import jax
import jax.numpy as jnp
import numpy as np
from jax import lax
from jax.experimental import pallas as pl
from jax.experimental.pallas import tpu as pltpu
from jax.sharding import PartitionSpec as P

PIX = 16
MESH = pl.DeviceIdType.MESH
NT = (((1,), (1,)), ((), ()))


def dft_table(samples, pixels):
    freqs = np.arange(pixels) - pixels / 2.0
    wave = np.exp(-2j * np.pi * freqs[:, None] * np.arange(samples)[None, :] / (2.0 * samples))
    kron = np.kron(wave, wave)
    return np.block([[kron.real, -kron.imag], [kron.imag, kron.real]]).astype(np.float32)


def poly_fit(func, degree):
    fit = np.polynomial.chebyshev.Chebyshev.interpolate(func, degree, domain=[0.0, 0.25])
    return [float(c) for c in fit.convert(kind=np.polynomial.Polynomial).coef]


def sin_over_r(z):
    return 2 * np.pi * np.sinc(2 * np.sqrt(z))


COS = poly_fit(lambda z: np.cos(2 * np.pi * np.sqrt(z)), 5)
SIN = poly_fit(sin_over_r, 5)


def horner(coefs, z):
    total = coefs[-1] * z + coefs[-2]
    for c in coefs[-3::-1]:
        total = total * z + c
    return total


def cos_sin(phase):
    turns = phase * (1.0 / (2.0 * math.pi))
    r = turns - jnp.round(turns)
    z = r * r
    return horner(COS, z), r * horner(SIN, z)


def column_sums(planes):
    pix = len(planes)
    run = planes[-1]
    nested = run
    for plane in planes[-2::-1]:
        run = run + plane
        nested = nested + run
    places = lax.broadcasted_iota(jnp.int32, run.shape, 0).astype(jnp.float32)
    centre = (pix - 1) / 2.0
    along_u = nested - (centre + 1.0) * run
    along_v = run * (places - centre)
    return [jnp.sum(x, axis=0, keepdims=True) for x in (run, along_u, along_v)]


def spot_rows(phase, real, imag, table):
    patterns = phase.shape[0]
    cs, sn = cos_sin(phase)
    even = jnp.concatenate([(cs * real).astype(jnp.bfloat16), (cs * imag).astype(jnp.bfloat16)], axis=1)
    odd = jnp.concatenate([(sn * -imag).astype(jnp.bfloat16), (sn * real).astype(jnp.bfloat16)], axis=1)
    field = jnp.concatenate([even, odd], axis=0)
    focal = lax.dot_general(table, field, NT, preferred_element_type=jnp.float32)
    half = focal.shape[0] // 2
    squares, crosses = [], []
    for u in range(PIX):
        re = focal[u * PIX:(u + 1) * PIX]
        im = focal[half + u * PIX:half + (u + 1) * PIX]
        c_re, s_re = re[:, :patterns], re[:, patterns:]
        c_im, s_im = im[:, :patterns], im[:, patterns:]
        squares.append((c_re * c_re + c_im * c_im) + (s_re * s_re + s_im * s_im))
        crosses.append(c_re * s_re + c_im * s_im)
    p0, pu, pv = column_sums(squares)
    q0, qu, qv = [2.0 * x for x in column_sums(crosses)]
    scale = 1.0 / ((p0 + q0) * (p0 - q0))
    return (qu * p0 - pu * q0) * scale, (qv * p0 - pv * q0) * scale


def diagonal_column(row):
    k = row.shape[1]
    shape = (k, k)
    same = lax.broadcasted_iota(jnp.int32, shape, 0) == lax.broadcasted_iota(jnp.int32, shape, 1)
    return jnp.sum(jnp.where(same, jnp.broadcast_to(row, shape), 0.0), axis=1, keepdims=True)


def commands_of(had, stroke):
    return (stroke * had.astype(jnp.float32).T).astype(jnp.bfloat16)


def slopes_kernel(
    n, chunks, per, flat,
    had_ref, stroke_ref, infl_ref, amp_ref, abe_ref, mask_ref, table_ref,
    out_ref,
    mid_buf, low_buf, up_buf, had_low, had_up, stroke_low, stroke_up, real, imag, rows,
    mid_sems, send_sems, recv_sems, cmd_send, cmd_recv,
):
    me = lax.axis_index("tile")
    has_low, has_up = me > 0, me < n - 1
    low_id, up_id = {"tile": jnp.maximum(me - 1, 0)}, {"tile": jnp.minimum(me + 1, n - 1)}
    width = per * flat
    barrier = pltpu.get_barrier_semaphore()

    @pl.when(has_low)
    def _():
        pl.semaphore_signal(barrier, inc=1, device_id=low_id, device_id_type=MESH)

    @pl.when(has_up)
    def _():
        pl.semaphore_signal(barrier, inc=1, device_id=up_id, device_id_type=MESH)

    def columns(c):
        return pl.ds(pl.multiple_of(c * width, width), width)

    def mid_copy(c):
        return pltpu.make_async_copy(infl_ref.at[1, :, columns(c)], mid_buf.at[c], mid_sems.at[c])

    def remote(src, dst, send, recv, device):
        return pltpu.make_async_remote_copy(
            src_ref=src, dst_ref=dst, send_sem=send, recv_sem=recv, device_id=device, device_id_type=MESH
        )

    def to_up(c):
        return remote(infl_ref.at[2, :, columns(c)], low_buf.at[c], send_sems.at[0, c], recv_sems.at[0, c], up_id)

    def to_low(c):
        return remote(infl_ref.at[0, :, columns(c)], up_buf.at[c], send_sems.at[1, c], recv_sems.at[1, c], low_id)

    def cmds_up():
        return (
            remote(had_ref, had_low, cmd_send.at[0], cmd_recv.at[0], up_id),
            remote(stroke_ref, stroke_low, cmd_send.at[1], cmd_recv.at[1], up_id),
        )

    def cmds_low():
        return (
            remote(had_ref, had_up, cmd_send.at[2], cmd_recv.at[2], low_id),
            remote(stroke_ref, stroke_up, cmd_send.at[3], cmd_recv.at[3], low_id),
        )

    inner = jnp.logical_and(has_low, has_up)

    @pl.when(inner)
    def _():
        pl.semaphore_wait(barrier, 2)

    @pl.when(jnp.logical_not(inner))
    def _():
        pl.semaphore_wait(barrier, 1)

    @pl.when(has_up)
    def _():
        for copy in cmds_up():
            copy.start()

    @pl.when(has_low)
    def _():
        for copy in cmds_low():
            copy.start()

    @pl.loop(0, chunks)
    def _(c):
        @pl.when(has_up)
        def _():
            to_up(c).start()

        @pl.when(has_low)
        def _():
            to_low(c).start()

        mid_copy(c).start()

    @pl.when(jnp.logical_not(has_low))
    def _():
        had_low[...] = jnp.zeros_like(had_low)
        stroke_low[...] = jnp.zeros_like(stroke_low)
        low_buf[...] = jnp.zeros_like(low_buf)

    @pl.when(jnp.logical_not(has_up))
    def _():
        had_up[...] = jnp.zeros_like(had_up)
        stroke_up[...] = jnp.zeros_like(stroke_up)
        up_buf[...] = jnp.zeros_like(up_buf)

    cs, sn = cos_sin(abe_ref[...])
    whole_real, whole_imag = (amp_ref[...] * cs).T, (amp_ref[...] * sn).T
    for c in range(chunks):
        real[c] = whole_real[c * per:(c + 1) * per]
        imag[c] = whole_imag[c * per:(c + 1) * per]

    @pl.when(has_up)
    def _():
        for copy in cmds_up():
            copy.wait_send()
        for copy in cmds_low():
            copy.wait_recv()

    @pl.when(has_low)
    def _():
        for copy in cmds_low():
            copy.wait_send()
        for copy in cmds_up():
            copy.wait_recv()

    mid_cmds = commands_of(had_ref[...], stroke_ref[...])
    low_cmds = commands_of(had_low[...], stroke_low[...])
    up_cmds = commands_of(had_up[...], stroke_up[...])

    @pl.loop(0, chunks)
    def _(c):
        mid_copy(c).wait()

        @pl.when(has_low)
        def _():
            to_up(c).wait_recv()

        @pl.when(has_up)
        def _():
            to_low(c).wait_recv()

        rows_u, rows_v = [], []
        for k in range(per):
            cols = slice(k * flat, (k + 1) * flat)
            phase = jnp.dot(low_cmds, low_buf[c, :, cols], preferred_element_type=jnp.float32)
            phase += jnp.dot(mid_cmds, mid_buf[c, :, cols], preferred_element_type=jnp.float32)
            phase += jnp.dot(up_cmds, up_buf[c, :, cols], preferred_element_type=jnp.float32)
            along_u, along_v = spot_rows(phase, real[c, k:k + 1, :], imag[c, k:k + 1, :], table_ref[...])
            rows_u.append(along_u)
            rows_v.append(along_v)
        rows[c, 0] = jnp.concatenate(rows_u, axis=0)
        rows[c, 1] = jnp.concatenate(rows_v, axis=0)

    mask = diagonal_column(mask_ref[...].astype(jnp.float32))
    for j in range(2):
        whole = jnp.concatenate([rows[c, j] for c in range(chunks)], axis=0)
        out_ref[j] = (whole * mask).astype(out_ref.dtype)

    @pl.loop(0, chunks)
    def _(c):
        @pl.when(has_up)
        def _():
            to_up(c).wait_send()

        @pl.when(has_low)
        def _():
            to_low(c).wait_send()


def gather_kernel(n, mine_ref, had_ref, stroke_ref, out_ref, held, own_sem, send_sems, recv_sems):
    me = lax.axis_index("tile")
    subs = mine_ref.shape[1]
    barrier = pltpu.get_barrier_semaphore()

    @pl.loop(1, n)
    def _(k):
        pl.semaphore_signal(barrier, inc=1, device_id={"tile": lax.rem(me + k, n)}, device_id_type=MESH)

    pl.semaphore_wait(barrier, n - 1)
    slot = held.at[:, pl.ds(pl.multiple_of(me * subs, subs), subs), :]
    own = pltpu.make_async_copy(mine_ref, slot, own_sem)
    own.start()

    def push(k):
        return pltpu.make_async_remote_copy(
            src_ref=mine_ref,
            dst_ref=slot,
            send_sem=send_sems.at[k],
            recv_sem=recv_sems.at[k],
            device_id={"tile": lax.rem(me + k, n)},
            device_id_type=MESH,
        )

    @pl.loop(1, n)
    def _(k):
        push(k).start()

    patterns = had_ref.shape[1]
    signs = had_ref[...].astype(jnp.float32).astype(jnp.bfloat16)
    scale = patterns * diagonal_column(stroke_ref[...])
    own.wait()

    @pl.loop(1, n)
    def _(k):
        push(k).wait()

    for c in range(2):
        summed = lax.dot_general(signs, held[c], NT, preferred_element_type=jnp.float32)
        out_ref[:, c, :] = summed / scale


def per_device(hadamard, stroke, influence, amplitude, aberration, valid_mask):
    n = lax.axis_size("tile")
    patterns, acts = hadamard.shape
    subs, samples = amplitude.shape[0], amplitude.shape[1]
    flat = samples * samples
    per = math.gcd(subs, 4)
    chunks = subs // per
    had = hadamard.T
    amp = amplitude.transpose(1, 2, 0).reshape(flat, subs)
    abe = aberration.transpose(1, 2, 0).reshape(flat, subs)
    stroke = stroke.reshape(1, acts)
    mask = valid_mask.reshape(1, subs)
    table = jnp.asarray(dft_table(samples, PIX), dtype=jnp.bfloat16)
    vmem = pl.BlockSpec(memory_space=pltpu.VMEM)
    slab = pltpu.VMEM((chunks, acts, per * flat), jnp.bfloat16)
    slopes = pl.pallas_call(
        functools.partial(slopes_kernel, n, chunks, per, flat),
        out_shape=jax.ShapeDtypeStruct((2, subs, patterns), jnp.bfloat16),
        in_specs=[vmem, vmem, pl.BlockSpec(memory_space=pltpu.HBM), vmem, vmem, vmem, vmem],
        out_specs=vmem,
        scratch_shapes=[
            slab, slab, slab,
            pltpu.VMEM((acts, patterns), jnp.int32),
            pltpu.VMEM((acts, patterns), jnp.int32),
            pltpu.VMEM((1, acts), jnp.float32),
            pltpu.VMEM((1, acts), jnp.float32),
            pltpu.VMEM((chunks, per, flat), jnp.float32),
            pltpu.VMEM((chunks, per, flat), jnp.float32),
            pltpu.VMEM((chunks, 2, per, patterns), jnp.float32),
            pltpu.SemaphoreType.DMA((chunks,)),
            pltpu.SemaphoreType.DMA((2, chunks)),
            pltpu.SemaphoreType.DMA((2, chunks)),
            pltpu.SemaphoreType.DMA((4,)),
            pltpu.SemaphoreType.DMA((4,)),
        ],
        compiler_params=pltpu.CompilerParams(
            collective_id=1, has_side_effects=True, vmem_limit_bytes=40 * 1024 * 1024
        ),
        name="slopes",
    )(had, stroke, influence, amp, abe, mask, table)
    return pl.pallas_call(
        functools.partial(gather_kernel, n),
        out_shape=jax.ShapeDtypeStruct((acts, 2, n * subs), jnp.float32),
        in_specs=[vmem] * 3,
        out_specs=vmem,
        scratch_shapes=[
            pltpu.VMEM((2, n * subs, patterns), jnp.bfloat16),
            pltpu.SemaphoreType.DMA,
            pltpu.SemaphoreType.DMA((n,)),
            pltpu.SemaphoreType.DMA((n,)),
        ],
        compiler_params=pltpu.CompilerParams(collective_id=0, has_side_effects=True),
        name="gather",
    )(slopes, had, stroke)


def solution(mesh):
    placed = (
        P(None, "tile"),
        P(("group", "tile")),
        P(None, ("group", "tile"), None),
        P(("group", "tile"), None, None),
        P(("group", "tile"), None, None),
        P(("group", "tile")),
    )
    return jax.shard_map(
        per_device,
        mesh=mesh,
        in_specs=placed,
        out_specs=P(("group", "tile"), None, None),
        check_vma=False,
    )
```

profile of v0, /device:TPU:0, one launch (start us, length us, event | category | flops | bytes accessed | tf_op | source)
XLA Modules:
  0.0 53.0 jit_solution(14319126017734123154)
XLA Ops:
  0.0 0.0 copy-start
  0.0 2.0 %copy-done = bf16[3,72,8192]{2,1,0:T(8,128)(2,1)S(1)} copy-done((bf16[3,72,8192]{2,1,0:T(8,128)(2,1)S(1)}, bf16[3,72,8192]{2,1,0:T(8,128)(2,1)}, u32[]{:S(2)}) %copy-start) | copy-done | bytes 3538968
  2.0 0.0 copy-start.1
  2.0 1.0 %copy-done.1 = bf16[512,512]{1,0:T(8,128)(2,1)S(1)} copy-done((bf16[512,512]{1,0:T(8,128)(2,1)S(1)}, bf16[512,512]{1,0:T(8,128)(2,1)}, u32[]{:S(2)}) %copy-start.1) | copy-done | bytes 524312
  3.0 0.0 copy-start.2
  3.0 0.8 %copy-done.2 = s32[128,72]{0,1:T(8,128)S(1)} copy-done((s32[128,72]{0,1:T(8,128)S(1)}, s32[128,72]{0,1:T(8,128)}, u32[]{:S(2)}) %copy-start.2) | copy-done | bytes 36888
  3.8 0.0 copy-start.3
  3.8 0.9 %copy-done.3 = f32[32,16,16]{0,2,1:T(8,128)S(1)} copy-done((f32[32,16,16]{0,2,1:T(8,128)S(1)}, f32[32,16,16]{0,2,1:T(8,128)}, u32[]{:S(2)}) %copy-start.3) | copy-done | bytes 32792
  4.7 0.0 copy-start.4
  4.7 0.9 %copy-done.4 = f32[32,16,16]{0,2,1:T(8,128)S(1)} copy-done((f32[32,16,16]{0,2,1:T(8,128)S(1)}, f32[32,16,16]{0,2,1:T(8,128)}, u32[]{:S(2)}) %copy-start.4) | copy-done | bytes 32792
  5.6 0.0 copy-start.6
  5.6 0.7 %copy-done.6 = f32[72]{0:T(128)S(1)} copy-done((f32[72]{0:T(128)S(1)}, f32[72]{0:T(128)}, u32[]{:S(2)}) %copy-start.6) | copy-done | bytes 312
  6.3 0.0 copy-start.7
  6.3 0.7 %copy-done.7 = s32[32]{0:T(128)S(1)} copy-done((s32[32]{0:T(128)S(1)}, s32[32]{0:T(128)}, u32[]{:S(2)}) %copy-start.7) | copy-done | bytes 152
  6.9 17.2 %slopes.1.mine_ref = bf16[2,32,128]{2,1,0:T(8,128)(2,1)S(1)} custom-call(s32[72,128]{1,0:T(8,128)S(1)} %bitcast.10, f32[1,72]{1,0:T(1,128)S(1)} %bitcast.14, bf16[3,72,8192]{2,1,0:T(8,128)(2,1)S(1)} %copy-done, f32[256,32]{1,0:T(8,128)S(1)} %bitcast.11, f32[256,32]{1,0:T(8,128)S(1)} %bitcast.12, s32[1,32]{1,0:T(1,128)S(1)} %bitcast.15, ...), custom_call_target="tpu_custom_call" | custom-call | tf_op jit(solution)/shard_map/slopes/pallas_call | solution.py:313
  24.1 0.0 copy-start.5
  24.1 0.6 %copy-done.5 = bf16[2,32,128]{2,1,0:T(8,128)(2,1)} copy-done((bf16[2,32,128]{2,1,0:T(8,128)(2,1)}, bf16[2,32,128]{2,1,0:T(8,128)(2,1)S(1)}, u32[]{:S(2)}) %copy-start.5) | copy-done | bytes 16408
  24.7 26.6 %gather.1 = f32[72,2,512]{2,1,0:T(2,128)} custom-call(bf16[2,32,128]{2,1,0:T(8,128)(2,1)} %copy-done.5, s32[72,128]{1,0:T(8,128)} %bitcast.9, f32[1,72]{1,0:T(1,128)} %bitcast.13), custom_call_target="tpu_custom_call" | custom-call | tf_op jit(solution)/shard_map/gather/pallas_call | solution.py:338
  51.3 1.7 %copy.9 = f32[72,2,512]{2,1,0:T(2,128)} copy(f32[72,2,512]{2,1,0:T(2,128)} %gather.1) | data formatting | bytes 589824
Async XLA Ops:
  0.0 2.0 %copy-start = (bf16[3,72,8192]{2,1,0:T(8,128)(2,1)S(1)}, bf16[3,72,8192]{2,1,0:T(8,128)(2,1)}, u32[]{:S(2)}) copy-start(bf16[3,72,8192]{2,1,0:T(8,128)(2,1)} %infl_ref.1) | copy-start | bytes 10616836
  2.0 1.0 %copy-start.1 = (bf16[512,512]{1,0:T(8,128)(2,1)S(1)}, bf16[512,512]{1,0:T(8,128)(2,1)}, u32[]{:S(2)}) copy-start(bf16[512,512]{1,0:T(8,128)(2,1)} %constant.2.clone.table_ref) | copy-start | bytes 1572868
  3.0 0.8 %copy-start.2 = (s32[128,72]{0,1:T(8,128)S(1)}, s32[128,72]{0,1:T(8,128)}, u32[]{:S(2)}) copy-start(s32[128,72]{0,1:T(8,128)} %param.7) | copy-start | bytes 110596
  3.8 0.9 %copy-start.3 = (f32[32,16,16]{0,2,1:T(8,128)S(1)}, f32[32,16,16]{0,2,1:T(8,128)}, u32[]{:S(2)}) copy-start(f32[32,16,16]{0,2,1:T(8,128)} %param.10) | copy-start | bytes 98308
  4.7 0.9 %copy-start.4 = (f32[32,16,16]{0,2,1:T(8,128)S(1)}, f32[32,16,16]{0,2,1:T(8,128)}, u32[]{:S(2)}) copy-start(f32[32,16,16]{0,2,1:T(8,128)} %param.11) | copy-start | bytes 98308
  5.6 0.7 %copy-start.6 = (f32[72]{0:T(128)S(1)}, f32[72]{0:T(128)}, u32[]{:S(2)}) copy-start(f32[72]{0:T(128)} %param.8) | copy-start | bytes 868
  6.3 0.7 %copy-start.7 = (s32[32]{0:T(128)S(1)}, s32[32]{0:T(128)}, u32[]{:S(2)}) copy-start(s32[32]{0:T(128)} %param.12) | copy-start | bytes 388
  24.1 0.6 %copy-start.5 = (bf16[2,32,128]{2,1,0:T(8,128)(2,1)}, bf16[2,32,128]{2,1,0:T(8,128)(2,1)S(1)}, u32[]{:S(2)}) copy-start(bf16[2,32,128]{2,1,0:T(8,128)(2,1)S(1)} %slopes.1.mine_ref) | copy-start | bytes 49156
where the time goes:
time: 53.4 us; the launch traced here: 53 us
  Pallas kernels  43.8 us (82%)
  local copies, waits for them, and re-layouts  9.22 us (17%)
    pallas_call x1, Pallas kernels, per_device(): pl.pallas_call(functools.partial(gather_kernel, n), out_shape=jax.ShapeDt...  26.6 us
    pallas_call x1, Pallas kernels, per_device(): pl.pallas_call(functools.partial(slopes_kernel, n, chunks, per, flat), ou...  17.2 us
    unnamed x17, local copies, waits for them, and re-layouts  9.22 us

commit v1 on v0

v1 whole, which is shorter than its diff:
```python
import functools
import math

import jax
import jax.numpy as jnp
import numpy as np
from jax import lax
from jax.experimental import pallas as pl
from jax.experimental.pallas import tpu as pltpu
from jax.sharding import PartitionSpec as P

PIX = 16
MESH = pl.DeviceIdType.MESH
NT = (((1,), (1,)), ((), ()))


def dft_table(samples, pixels):
    freqs = np.arange(pixels) - pixels / 2.0
    wave = np.exp(-2j * np.pi * freqs[:, None] * np.arange(samples)[None, :] / (2.0 * samples))
    kron = np.kron(wave, wave)
    return np.block([[kron.real, -kron.imag], [kron.imag, kron.real]]).astype(np.float32)


def poly_fit(func, degree):
    fit = np.polynomial.chebyshev.Chebyshev.interpolate(func, degree, domain=[0.0, 0.25])
    return [float(c) for c in fit.convert(kind=np.polynomial.Polynomial).coef]


def sin_over_r(z):
    return 2 * np.pi * np.sinc(2 * np.sqrt(z))


COS = poly_fit(lambda z: np.cos(2 * np.pi * np.sqrt(z)), 5)
SIN = poly_fit(sin_over_r, 5)


def horner(coefs, z):
    total = coefs[-1] * z + coefs[-2]
    for c in coefs[-3::-1]:
        total = total * z + c
    return total


def cos_sin(phase):
    turns = phase * (1.0 / (2.0 * math.pi))
    r = turns - jnp.round(turns)
    z = r * r
    return horner(COS, z), r * horner(SIN, z)


def column_sums(planes):
    pix = len(planes)
    run = planes[-1]
    nested = run
    for plane in planes[-2::-1]:
        run = run + plane
        nested = nested + run
    places = lax.broadcasted_iota(jnp.int32, run.shape, 0).astype(jnp.float32)
    centre = (pix - 1) / 2.0
    along_u = nested - (centre + 1.0) * run
    along_v = run * (places - centre)
    return [jnp.sum(x, axis=0, keepdims=True) for x in (run, along_u, along_v)]


def spot_rows(phase, real, imag, table):
    patterns = phase.shape[0]
    cs, sn = cos_sin(phase)
    even = jnp.concatenate([(cs * real).astype(jnp.bfloat16), (cs * imag).astype(jnp.bfloat16)], axis=1)
    odd = jnp.concatenate([(sn * -imag).astype(jnp.bfloat16), (sn * real).astype(jnp.bfloat16)], axis=1)
    field = jnp.concatenate([even, odd], axis=0)
    focal = lax.dot_general(table, field, NT, preferred_element_type=jnp.float32)
    half = focal.shape[0] // 2
    squares, crosses = [], []
    for u in range(PIX):
        re = focal[u * PIX:(u + 1) * PIX]
        im = focal[half + u * PIX:half + (u + 1) * PIX]
        c_re, s_re = re[:, :patterns], re[:, patterns:]
        c_im, s_im = im[:, :patterns], im[:, patterns:]
        squares.append((c_re * c_re + c_im * c_im) + (s_re * s_re + s_im * s_im))
        crosses.append(c_re * s_re + c_im * s_im)
    p0, pu, pv = column_sums(squares)
    q0, qu, qv = [2.0 * x for x in column_sums(crosses)]
    scale = 1.0 / ((p0 + q0) * (p0 - q0))
    return (qu * p0 - pu * q0) * scale, (qv * p0 - pv * q0) * scale


def diagonal_column(row):
    k = row.shape[1]
    shape = (k, k)
    same = lax.broadcasted_iota(jnp.int32, shape, 0) == lax.broadcasted_iota(jnp.int32, shape, 1)
    return jnp.sum(jnp.where(same, jnp.broadcast_to(row, shape), 0.0), axis=1, keepdims=True)


def slopes_kernel(
    n, chunks, per, flat, parts,
    had_hbm, stroke_hbm, infl_ref, amp_hbm, abe_hbm, mask_hbm, table_hbm,
    held_ref,
    had, stroke, amp, abe, mask, table,
    mid_buf, low_buf, up_buf, cmds, cmds_low, cmds_up, real, imag, rows, mine,
    load_sems, mid_sems, send_sems, recv_sems, cmd_send, cmd_recv, own_sems, push_send, push_recv,
):
    me = lax.axis_index("tile")
    has_low, has_up = me > 0, me < n - 1
    low_id, up_id = {"tile": jnp.maximum(me - 1, 0)}, {"tile": jnp.minimum(me + 1, n - 1)}
    width = per * flat
    subs = mine.shape[1]
    part = subs // parts
    barrier = pltpu.get_barrier_semaphore()

    @pl.loop(1, n)
    def _(k):
        pl.semaphore_signal(barrier, inc=1, device_id={"tile": lax.rem(me + k, n)}, device_id_type=MESH)

    def columns(c):
        return pl.ds(pl.multiple_of(c * width, width), width)

    def mid_copy(c):
        return pltpu.make_async_copy(infl_ref.at[1, :, columns(c)], mid_buf.at[c], mid_sems.at[c])

    def remote(src, dst, send, recv, device):
        return pltpu.make_async_remote_copy(
            src_ref=src, dst_ref=dst, send_sem=send, recv_sem=recv, device_id=device, device_id_type=MESH
        )

    def to_up(c):
        return remote(infl_ref.at[2, :, columns(c)], low_buf.at[c], send_sems.at[0, c], recv_sems.at[0, c], up_id)

    def to_low(c):
        return remote(infl_ref.at[0, :, columns(c)], up_buf.at[c], send_sems.at[1, c], recv_sems.at[1, c], low_id)

    def cmds_to_up():
        return remote(cmds, cmds_low, cmd_send.at[0], cmd_recv.at[0], up_id)

    def cmds_to_low():
        return remote(cmds, cmds_up, cmd_send.at[1], cmd_recv.at[1], low_id)

    loads = [
        pltpu.make_async_copy(src, dst, load_sems.at[k])
        for k, (src, dst) in enumerate([
            (had_hbm, had), (stroke_hbm, stroke), (abe_hbm, abe), (amp_hbm, amp), (mask_hbm, mask), (table_hbm, table),
        ])
    ]
    for load in loads:
        load.start()

    @pl.loop(0, chunks)
    def _(c):
        mid_copy(c).start()

    loads[0].wait()
    loads[1].wait()
    cmds[...] = (had[...].astype(jnp.float32) * diagonal_column(stroke[...])).astype(jnp.bfloat16)

    pl.semaphore_wait(barrier, n - 1)

    @pl.when(has_up)
    def _():
        cmds_to_up().start()

    @pl.when(has_low)
    def _():
        cmds_to_low().start()

    @pl.loop(0, chunks)
    def _(c):
        @pl.when(has_up)
        def _():
            to_up(c).start()

        @pl.when(has_low)
        def _():
            to_low(c).start()

    @pl.when(jnp.logical_not(has_low))
    def _():
        cmds_low[...] = jnp.zeros_like(cmds_low)
        low_buf[...] = jnp.zeros_like(low_buf)

    @pl.when(jnp.logical_not(has_up))
    def _():
        cmds_up[...] = jnp.zeros_like(cmds_up)
        up_buf[...] = jnp.zeros_like(up_buf)

    for load in loads[2:]:
        load.wait()
    cs, sn = cos_sin(abe[...])
    whole_real, whole_imag = (amp[...] * cs).T, (amp[...] * sn).T
    for c in range(chunks):
        real[c] = whole_real[c * per:(c + 1) * per]
        imag[c] = whole_imag[c * per:(c + 1) * per]
    mask_column = diagonal_column(mask[...].astype(jnp.float32))

    @pl.when(has_up)
    def _():
        cmds_to_up().wait_send()
        cmds_to_low().wait_recv()

    @pl.when(has_low)
    def _():
        cmds_to_low().wait_send()
        cmds_to_up().wait_recv()

    mid_cmds = cmds[...].T
    low_cmds = cmds_low[...].T
    up_cmds = cmds_up[...].T

    def slot(g):
        return held_ref.at[:, pl.ds(pl.multiple_of(me * subs + g * part, part), part), :]

    def piece(g):
        return mine.at[:, pl.ds(g * part, part), :]

    def own(g):
        return pltpu.make_async_copy(piece(g), slot(g), own_sems.at[g])

    def push(g, k):
        return remote(piece(g), slot(g), push_send.at[g, k], push_recv.at[g, k], {"tile": lax.rem(me + k, n)})

    steps = chunks // parts
    for g in range(parts):
        @pl.loop(g * steps, (g + 1) * steps)
        def _(c):
            mid_copy(c).wait()

            @pl.when(has_low)
            def _():
                to_up(c).wait_recv()

            @pl.when(has_up)
            def _():
                to_low(c).wait_recv()

            rows_u, rows_v = [], []
            for k in range(per):
                cols = slice(k * flat, (k + 1) * flat)
                phase = jnp.dot(low_cmds, low_buf[c, :, cols], preferred_element_type=jnp.float32)
                phase += jnp.dot(mid_cmds, mid_buf[c, :, cols], preferred_element_type=jnp.float32)
                phase += jnp.dot(up_cmds, up_buf[c, :, cols], preferred_element_type=jnp.float32)
                along_u, along_v = spot_rows(phase, real[c, k:k + 1, :], imag[c, k:k + 1, :], table[...])
                rows_u.append(along_u)
                rows_v.append(along_v)
            rows[c, 0] = jnp.concatenate(rows_u, axis=0)
            rows[c, 1] = jnp.concatenate(rows_v, axis=0)

        for j in range(2):
            whole = jnp.concatenate([rows[c, j] for c in range(g * steps, (g + 1) * steps)], axis=0)
            mine[j, g * part:(g + 1) * part] = (whole * mask_column[g * part:(g + 1) * part]).astype(mine.dtype)
        own(g).start()

        @pl.loop(1, n)
        def _(k):
            push(g, k).start()

    @pl.loop(0, chunks)
    def _(c):
        @pl.when(has_up)
        def _():
            to_up(c).wait_send()

        @pl.when(has_low)
        def _():
            to_low(c).wait_send()

    for g in range(parts):
        own(g).wait()

        @pl.loop(1, n)
        def _(k):
            push(g, k).wait()


def apply_kernel(held, had_ref, stroke_ref, out_ref):
    patterns = had_ref.shape[1]
    signs = had_ref[...].astype(jnp.float32).astype(jnp.bfloat16)
    scale = patterns * diagonal_column(stroke_ref[...])
    for c in range(2):
        summed = lax.dot_general(signs, held[c], NT, preferred_element_type=jnp.float32)
        out_ref[:, c, :] = summed / scale


def per_device(hadamard, stroke, influence, amplitude, aberration, valid_mask):
    n = lax.axis_size("tile")
    patterns, acts = hadamard.shape
    subs, samples = amplitude.shape[0], amplitude.shape[1]
    flat = samples * samples
    per = math.gcd(subs, 2)
    chunks = subs // per
    parts = 2 if subs % 32 == 0 else 1
    had = hadamard.T
    amp = amplitude.transpose(1, 2, 0).reshape(flat, subs)
    abe = aberration.transpose(1, 2, 0).reshape(flat, subs)
    stroke = stroke.reshape(1, acts)
    mask = valid_mask.reshape(1, subs)
    table = jnp.asarray(dft_table(samples, PIX), dtype=jnp.bfloat16)
    vmem = pl.BlockSpec(memory_space=pltpu.VMEM)
    hbm = pl.BlockSpec(memory_space=pltpu.HBM)
    slab = pltpu.VMEM((chunks, acts, per * flat), jnp.bfloat16)
    held = pl.pallas_call(
        functools.partial(slopes_kernel, n, chunks, per, flat, parts),
        out_shape=jax.ShapeDtypeStruct((2, n * subs, patterns), jnp.bfloat16),
        in_specs=[hbm] * 7,
        out_specs=vmem,
        scratch_shapes=[
            pltpu.VMEM((acts, patterns), jnp.int32),
            pltpu.VMEM((1, acts), jnp.float32),
            pltpu.VMEM((flat, subs), jnp.float32),
            pltpu.VMEM((flat, subs), jnp.float32),
            pltpu.VMEM((1, subs), jnp.int32),
            pltpu.VMEM(table.shape, jnp.bfloat16),
            slab, slab, slab,
            pltpu.VMEM((acts, patterns), jnp.bfloat16),
            pltpu.VMEM((acts, patterns), jnp.bfloat16),
            pltpu.VMEM((acts, patterns), jnp.bfloat16),
            pltpu.VMEM((chunks, per, flat), jnp.float32),
            pltpu.VMEM((chunks, per, flat), jnp.float32),
            pltpu.VMEM((chunks, 2, per, patterns), jnp.float32),
            pltpu.VMEM((2, subs, patterns), jnp.bfloat16),
            pltpu.SemaphoreType.DMA((6,)),
            pltpu.SemaphoreType.DMA((chunks,)),
            pltpu.SemaphoreType.DMA((2, chunks)),
            pltpu.SemaphoreType.DMA((2, chunks)),
            pltpu.SemaphoreType.DMA((2,)),
            pltpu.SemaphoreType.DMA((2,)),
            pltpu.SemaphoreType.DMA((parts,)),
            pltpu.SemaphoreType.DMA((parts, n)),
            pltpu.SemaphoreType.DMA((parts, n)),
        ],
        compiler_params=pltpu.CompilerParams(
            collective_id=1, has_side_effects=True, vmem_limit_bytes=62 * 1024 * 1024
        ),
        name="slopes",
    )(had, stroke, influence, amp, abe, mask, table)
    return pl.pallas_call(
        apply_kernel,
        out_shape=jax.ShapeDtypeStruct((acts, 2, n * subs), jnp.float32),
        in_specs=[vmem] * 3,
        out_specs=vmem,
        name="apply",
    )(held, had, stroke)


def solution(mesh):
    placed = (
        P(None, "tile"),
        P(("group", "tile")),
        P(None, ("group", "tile"), None),
        P(("group", "tile"), None, None),
        P(("group", "tile"), None, None),
        P(("group", "tile")),
    )
    return jax.shard_map(
        per_device,
        mesh=mesh,
        in_specs=placed,
        out_specs=P(("group", "tile"), None, None),
        check_vma=False,
    )
```

time: 53.4 us -> 44.6 us (0.84)
  local copies, waits for them, and re-layouts: 9.22 us -> 0 us
  Pallas kernels: 43.8 us -> 44.4 us
    unnamed x17 -> x0, local copies, waits for them, and re-layouts: 9.22 us -> none
    pallas_call x2, Pallas kernels: 43.8 us -> 44.4 us  [the longest x1 42.5 us: per_device(): pl.pallas_call(functools.partial(slopes_kernel, n, chunks, per, flat, par...]
where the time goes in v1:
time: 44.6 us; the launch traced here: 44.5 us
  Pallas kernels  44.4 us (100%)
    pallas_call x1, Pallas kernels, per_device(): pl.pallas_call(functools.partial(slopes_kernel, n, chunks, per, flat, par...  42.5 us
    pallas_call x1, Pallas kernels, per_device(): pl.pallas_call(apply_kernel, out_shape=jax.ShapeDtypeStruct((acts, 2, n *...  1.92 us

profile of v1, /device:TPU:0, one launch (start us, length us, event | category | flops | bytes accessed | tf_op | source)
XLA Modules:
  0.0 44.5 jit_solution(4417729198618148221)
XLA Ops:
  0.0 42.5 %slopes.1.held = bf16[2,512,128]{2,1,0:T(8,128)(2,1)} custom-call(s32[72,128]{1,0:T(8,128)} %bitcast.9, f32[1,72]{1,0:T(1,128)} %bitcast.13, bf16[3,72,8192]{2,1,0:T(8,128)(2,1)} %infl_ref.1, f32[256,32]{1,0:T(8,128)} %bitcast.11, f32[256,32]{1,0:T(8,128)} %bitcast.12, s32[1,32]{1,0:T(1,128)} %bitcast.15, bf16[512,512]{1,0:T(8,128)(2,1)} %constant.2.clone.table_hbm), custom_call_target="tpu_custom_call" | custom-call | tf_op jit(solution)/shard_map/slopes/pallas_call | solution.py:298
  42.5 1.9 %apply.1 = f32[72,2,512]{2,1,0:T(2,128)} custom-call(bf16[2,512,128]{2,1,0:T(8,128)(2,1)} %slopes.1.held, s32[72,128]{1,0:T(8,128)} %bitcast.10, f32[1,72]{1,0:T(1,128)} %bitcast.14), custom_call_target="tpu_custom_call" | custom-call | tf_op jit(solution)/shard_map/apply/pallas_call | solution.py:333

commit v2 on v1

--- a/solution.py
+++ b/solution.py
@@ -10,6 +10,10 @@
 from jax.sharding import PartitionSpec as P
 
 PIX = 16
+NEAR = 4
+FAR = 6
+AHEAD = 3
+BIAS = 8
 MESH = pl.DeviceIdType.MESH
 NT = (((1,), (1,)), ((), ()))
 
@@ -92,24 +96,63 @@
 
 
 def slopes_kernel(
-    n, chunks, per, flat, parts,
+    n, relays, chunks, per, flat, parts,
     had_hbm, stroke_hbm, infl_ref, amp_hbm, abe_hbm, mask_hbm, table_hbm,
     held_ref,
     had, stroke, amp, abe, mask, table,
-    mid_buf, low_buf, up_buf, cmds, cmds_low, cmds_up, real, imag, rows, mine,
-    load_sems, mid_sems, send_sems, recv_sems, cmd_send, cmd_recv, own_sems, push_send, push_recv,
+    mid_buf, low_buf, up_buf, cmds, cmds_low, cmds_up, real, imag, rows, mask_rows, mine, passing,
+    load_sems, mid_sems, send_sems, recv_sems, cmd_send, cmd_recv, own_sems, push_send, push_recv, known, pass_send, pass_recv,
 ):
     me = lax.axis_index("tile")
     has_low, has_up = me > 0, me < n - 1
     low_id, up_id = {"tile": jnp.maximum(me - 1, 0)}, {"tile": jnp.minimum(me + 1, n - 1)}
     width = per * flat
-    subs = mine.shape[1]
-    part = subs // parts
+    part = mine.shape[2]
+    subs = parts * part
+    steps = chunks // parts
+    rounds = (n - 1).bit_length()
+    span_up = jnp.where(lax.rem(me, 4) == 3, FAR, NEAR)
+    span_low = jnp.where(lax.rem(me, 4) == 0, FAR, NEAR)
     barrier = pltpu.get_barrier_semaphore()
 
-    @pl.loop(1, n)
-    def _(k):
-        pl.semaphore_signal(barrier, inc=1, device_id={"tile": lax.rem(me + k, n)}, device_id_type=MESH)
+    def greet(sem, distance):
+        @pl.when(me >= distance)
+        def _():
+            pl.semaphore_signal(sem, inc=1, device_id={"tile": me - distance}, device_id_type=MESH)
+
+        @pl.when(me < n - distance)
+        def _():
+            pl.semaphore_signal(sem, inc=1, device_id={"tile": me + distance}, device_id_type=MESH)
+
+    def met(sem, distance):
+        both = jnp.logical_and(me >= distance, me < n - distance)
+        either = jnp.logical_or(me >= distance, me < n - distance)
+
+        @pl.when(both)
+        def _():
+            pl.semaphore_wait(sem, 2)
+
+        @pl.when(jnp.logical_and(either, jnp.logical_not(both)))
+        def _():
+            pl.semaphore_wait(sem, 1)
+
+    place = lax.rem(me, 4)
+    levels = n // 4
+    far_up = jnp.logical_and(place == 3, has_up)
+    far_low = jnp.logical_and(place == 0, has_low)
+    pass_up = jnp.logical_and(place == 1, me + 3 < n)
+    pass_low = jnp.logical_and(place == 2, me >= 3)
+
+    def salute(condition, offset):
+        @pl.when(condition)
+        def _():
+            pl.semaphore_signal(barrier, inc=1, device_id={"tile": me + offset}, device_id_type=MESH)
+
+    greet(barrier, 1)
+    if relays:
+        for condition, offsets in ((far_up, (-2, 3)), (far_low, (2, -3)), (pass_up, (2, 3)), (pass_low, (-2, -3))):
+            for offset in offsets:
+                salute(condition, offset)
 
     def columns(c):
         return pl.ds(pl.multiple_of(c * width, width), width)
@@ -121,6 +164,53 @@
         return pltpu.make_async_remote_copy(
             src_ref=src, dst_ref=dst, send_sem=send, recv_sem=recv, device_id=device, device_id_type=MESH
         )
+
+    def detour(level, c, count_up):
+        low = chunks * (level + 1) // levels - chunks // BIAS
+        count = chunks - low if count_up else low
+        return ((c + 1) * count) // chunks != (c * count) // chunks
+
+    def via_up(t, c):
+        return detour(t // 4, c, True)
+
+    def via_low(t, c):
+        return detour(t // 4 - 1, c, False)
+
+    def aside_up(c):
+        source = infl_ref.at[2, :, columns(c)]
+        return remote(source, passing.at[c], send_sems.at[0, c], pass_recv.at[c], {"tile": jnp.maximum(me - 2, 0)})
+
+    def aside_low(c):
+        source = infl_ref.at[0, :, columns(c)]
+        return remote(source, passing.at[c], send_sems.at[1, c], pass_recv.at[c], {"tile": jnp.minimum(me + 2, n - 1)})
+
+    def onward_up(c):
+        target = {"tile": jnp.minimum(me + 3, n - 1)}
+        return remote(passing.at[c], low_buf.at[c], pass_send.at[c], recv_sems.at[0, c], target)
+
+    def onward_low(c):
+        target = {"tile": jnp.maximum(me - 3, 0)}
+        return remote(passing.at[c], up_buf.at[c], pass_send.at[c], recv_sems.at[1, c], target)
+
+    def relay(c):
+        @pl.when(jnp.logical_and(pass_up, via_up(me + 2, c)))
+        def _():
+            aside_up(c).wait_recv()
+            onward_up(c).start()
+
+        @pl.when(jnp.logical_and(pass_low, via_low(me - 2, c)))
+        def _():
+            aside_low(c).wait_recv()
+            onward_low(c).start()
+
+    def relay_done(c):
+        @pl.when(jnp.logical_and(pass_up, via_up(me + 2, c)))
+        def _():
+            onward_up(c).wait_send()
+
+        @pl.when(jnp.logical_and(pass_low, via_low(me - 2, c)))
+        def _():
+            onward_low(c).wait_send()
 
     def to_up(c):
         return remote(infl_ref.at[2, :, columns(c)], low_buf.at[c], send_sems.at[0, c], recv_sems.at[0, c], up_id)
@@ -143,33 +233,56 @@
     for load in loads:
         load.start()
 
+    peers = has_low.astype(jnp.int32) + has_up.astype(jnp.int32)
+    if relays:
+        for condition in (far_up, far_low, pass_up, pass_low):
+            peers += 2 * condition.astype(jnp.int32)
+    pl.semaphore_wait(barrier, peers)
+
+    def send_to(exists, far, span, c, straight, aside, via):
+        m = c + span
+        go = jnp.logical_and(exists, jnp.logical_and(m >= 0, m < chunks))
+        around = jnp.logical_and(far, via(me, m)) if relays else False
+
+        @pl.when(jnp.logical_and(go, jnp.logical_not(around)))
+        def _():
+            straight(m).start()
+
+        if relays:
+            @pl.when(jnp.logical_and(go, around))
+            def _():
+                aside(m).start()
+
+    def send_slab(c):
+        send_to(has_up, far_up, span_up, c, to_up, aside_up, via_up)
+        send_to(has_low, far_low, span_low, c, to_low, aside_low, via_low)
+
+    first = -max(NEAR, FAR)
+
+    @pl.loop(first, first + 2)
+    def _(c):
+        send_slab(c)
+
+    greet(known.at[0], 1)
+    loads[0].wait()
+    loads[1].wait()
+    cmds[...] = (had[...].astype(jnp.float32) * diagonal_column(stroke[...])).astype(jnp.bfloat16)
+
+    @pl.when(has_up)
+    def _():
+        cmds_to_up().start()
+
+    @pl.when(has_low)
+    def _():
+        cmds_to_low().start()
+
+    @pl.loop(first + 2, 0)
+    def _(c):
+        send_slab(c)
+
     @pl.loop(0, chunks)
     def _(c):
         mid_copy(c).start()
-
-    loads[0].wait()
-    loads[1].wait()
-    cmds[...] = (had[...].astype(jnp.float32) * diagonal_column(stroke[...])).astype(jnp.bfloat16)
-
-    pl.semaphore_wait(barrier, n - 1)
-
-    @pl.when(has_up)
-    def _():
-        cmds_to_up().start()
-
-    @pl.when(has_low)
-    def _():
-        cmds_to_low().start()
-
-    @pl.loop(0, chunks)
-    def _(c):
-        @pl.when(has_up)
-        def _():
-            to_up(c).start()
-
-        @pl.when(has_low)
-        def _():
-            to_low(c).start()
 
     @pl.when(jnp.logical_not(has_low))
     def _():
@@ -189,6 +302,8 @@
         real[c] = whole_real[c * per:(c + 1) * per]
         imag[c] = whole_imag[c * per:(c + 1) * per]
     mask_column = diagonal_column(mask[...].astype(jnp.float32))
+    for g in range(parts):
+        mask_rows[g] = jnp.broadcast_to(mask_column[g * part:(g + 1) * part], mask_rows.shape[1:])
 
     @pl.when(has_up)
     def _():
@@ -200,6 +315,11 @@
         cmds_to_low().wait_send()
         cmds_to_up().wait_recv()
 
+    if relays:
+        @pl.loop(0, AHEAD)
+        def _(c):
+            relay(c)
+
     mid_cmds = cmds[...].T
     low_cmds = cmds_low[...].T
     up_cmds = cmds_up[...].T
@@ -207,49 +327,60 @@
     def slot(g):
         return held_ref.at[:, pl.ds(pl.multiple_of(me * subs + g * part, part), part), :]
 
-    def piece(g):
-        return mine.at[:, pl.ds(g * part, part), :]
-
     def own(g):
-        return pltpu.make_async_copy(piece(g), slot(g), own_sems.at[g])
+        return pltpu.make_async_copy(mine.at[g], slot(g), own_sems.at[g])
 
     def push(g, k):
-        return remote(piece(g), slot(g), push_send.at[g, k], push_recv.at[g, k], {"tile": lax.rem(me + k, n)})
-
-    steps = chunks // parts
-    for g in range(parts):
-        @pl.loop(g * steps, (g + 1) * steps)
-        def _(c):
-            mid_copy(c).wait()
-
-            @pl.when(has_low)
+        return remote(mine.at[g], slot(g), push_send.at[g, k], push_recv.at[g, k], {"tile": lax.rem(me + k, n)})
+
+    @pl.loop(0, chunks)
+    def _(c):
+        mid_copy(c).wait()
+
+        @pl.when(has_low)
+        def _():
+            to_up(c).wait_recv()
+
+        @pl.when(has_up)
+        def _():
+            to_low(c).wait_recv()
+
+        send_slab(c)
+        if relays:
+            @pl.when(c + AHEAD < chunks)
             def _():
-                to_up(c).wait_recv()
-
-            @pl.when(has_up)
+                relay(c + AHEAD)
+
+        rows_u, rows_v = [], []
+        for k in range(per):
+            cols = slice(k * flat, (k + 1) * flat)
+            phase = jnp.dot(low_cmds, low_buf[c, :, cols], preferred_element_type=jnp.float32)
+            phase += jnp.dot(mid_cmds, mid_buf[c, :, cols], preferred_element_type=jnp.float32)
+            phase += jnp.dot(up_cmds, up_buf[c, :, cols], preferred_element_type=jnp.float32)
+            along_u, along_v = spot_rows(phase, real[c, k:k + 1, :], imag[c, k:k + 1, :], table[...])
+            rows_u.append(along_u)
+            rows_v.append(along_v)
+        rows[c, 0] = jnp.concatenate(rows_u, axis=0)
+        rows[c, 1] = jnp.concatenate(rows_v, axis=0)
+
+        for r in range(rounds):
+            @pl.when(c == r * steps // rounds)
             def _():
-                to_low(c).wait_recv()
-
-            rows_u, rows_v = [], []
-            for k in range(per):
-                cols = slice(k * flat, (k + 1) * flat)
-                phase = jnp.dot(low_cmds, low_buf[c, :, cols], preferred_element_type=jnp.float32)
-                phase += jnp.dot(mid_cmds, mid_buf[c, :, cols], preferred_element_type=jnp.float32)
-                phase += jnp.dot(up_cmds, up_buf[c, :, cols], preferred_element_type=jnp.float32)
-                along_u, along_v = spot_rows(phase, real[c, k:k + 1, :], imag[c, k:k + 1, :], table[...])
-                rows_u.append(along_u)
-                rows_v.append(along_v)
-            rows[c, 0] = jnp.concatenate(rows_u, axis=0)
-            rows[c, 1] = jnp.concatenate(rows_v, axis=0)
-
-        for j in range(2):
-            whole = jnp.concatenate([rows[c, j] for c in range(g * steps, (g + 1) * steps)], axis=0)
-            mine[j, g * part:(g + 1) * part] = (whole * mask_column[g * part:(g + 1) * part]).astype(mine.dtype)
-        own(g).start()
-
-        @pl.loop(1, n)
-        def _(k):
-            push(g, k).start()
+                met(known.at[r], 2 ** r)
+                if r + 1 < rounds:
+                    greet(known.at[r + 1], 2 ** (r + 1))
+
+        @pl.when(lax.rem(c, steps) == steps - 1)
+        def _():
+            g = c // steps
+            for j in range(2):
+                whole = jnp.concatenate([rows[g * steps + i, j] for i in range(steps)], axis=0)
+                mine[g, j] = (whole * mask_rows[g]).astype(mine.dtype)
+            own(g).start()
+
+            @pl.loop(1, n)
+            def _(k):
+                push(g, k).start()
 
     @pl.loop(0, chunks)
     def _(c):
@@ -261,7 +392,11 @@
         def _():
             to_low(c).wait_send()
 
-    for g in range(parts):
+        if relays:
+            relay_done(c)
+
+    @pl.loop(0, parts)
+    def _(g):
         own(g).wait()
 
         @pl.loop(1, n)
@@ -278,14 +413,14 @@
         out_ref[:, c, :] = summed / scale
 
 
-def per_device(hadamard, stroke, influence, amplitude, aberration, valid_mask):
+def per_device(relays, hadamard, stroke, influence, amplitude, aberration, valid_mask):
     n = lax.axis_size("tile")
     patterns, acts = hadamard.shape
     subs, samples = amplitude.shape[0], amplitude.shape[1]
     flat = samples * samples
     per = math.gcd(subs, 2)
     chunks = subs // per
-    parts = 2 if subs % 32 == 0 else 1
+    parts = subs // 8 if subs % 8 == 0 else 1
     had = hadamard.T
     amp = amplitude.transpose(1, 2, 0).reshape(flat, subs)
     abe = aberration.transpose(1, 2, 0).reshape(flat, subs)
@@ -296,10 +431,10 @@
     hbm = pl.BlockSpec(memory_space=pltpu.HBM)
     slab = pltpu.VMEM((chunks, acts, per * flat), jnp.bfloat16)
     held = pl.pallas_call(
-        functools.partial(slopes_kernel, n, chunks, per, flat, parts),
+        functools.partial(slopes_kernel, n, relays, chunks, per, flat, parts),
         out_shape=jax.ShapeDtypeStruct((2, n * subs, patterns), jnp.bfloat16),
         in_specs=[hbm] * 7,
-        out_specs=vmem,
+        out_specs=hbm,
         scratch_shapes=[
             pltpu.VMEM((acts, patterns), jnp.int32),
             pltpu.VMEM((1, acts), jnp.float32),
@@ -314,7 +449,9 @@
             pltpu.VMEM((chunks, per, flat), jnp.float32),
             pltpu.VMEM((chunks, per, flat), jnp.float32),
             pltpu.VMEM((chunks, 2, per, patterns), jnp.float32),
-            pltpu.VMEM((2, subs, patterns), jnp.bfloat16),
+            pltpu.VMEM((parts, subs // parts, patterns), jnp.float32),
+            pltpu.VMEM((parts, 2, subs // parts, patterns), jnp.bfloat16),
+            slab if relays else pltpu.VMEM((8, 128), jnp.bfloat16),
             pltpu.SemaphoreType.DMA((6,)),
             pltpu.SemaphoreType.DMA((chunks,)),
             pltpu.SemaphoreType.DMA((2, chunks)),
@@ -324,6 +461,9 @@
             pltpu.SemaphoreType.DMA((parts,)),
             pltpu.SemaphoreType.DMA((parts, n)),
             pltpu.SemaphoreType.DMA((parts, n)),
+            pltpu.SemaphoreType.REGULAR(((n - 1).bit_length(),)),
+            pltpu.SemaphoreType.DMA((chunks,)),
+            pltpu.SemaphoreType.DMA((chunks,)),
         ],
         compiler_params=pltpu.CompilerParams(
             collective_id=1, has_side_effects=True, vmem_limit_bytes=62 * 1024 * 1024
@@ -339,6 +479,24 @@
     )(held, had, stroke)
 
 
+def hops(mesh, a, b):
+    first, second = (getattr(mesh.devices[0, t], "coords", None) for t in (a, b))
+    if first is None or second is None:
+        return 0
+    return sum(abs(p - q) for p, q in zip(first, second))
+
+
+def relays_fit(mesh):
+    n = mesh.shape["tile"]
+    if mesh.axis_names != ("group", "tile") or n % 4 or n < 8:
+        return False
+    for t in range(3, n - 1, 4):
+        path = [(t, t + 1, 2), (t, t - 2, 1), (t - 2, t + 1, 1), (t + 1, t + 3, 1), (t + 3, t, 1)]
+        if any(hops(mesh, a, b) != count for a, b, count in path):
+            return False
+    return True
+
+
 def solution(mesh):
     placed = (
         P(None, "tile"),
@@ -349,7 +507,7 @@
         P(("group", "tile")),
     )
     return jax.shard_map(
-        per_device,
+        functools.partial(per_device, relays_fit(mesh)),
         mesh=mesh,
         in_specs=placed,
         out_specs=P(("group", "tile"), None, None),

time: 44.6 us -> 40.4 us (0.906)
  Pallas kernels: 44.4 us -> 40.2 us
    pallas_call x1, Pallas kernels: 42.5 us -> 38.3 us  [per_device(): pl.pallas_call(functools.partial(slopes_kernel, n, relays, chunks, per, f...]
where the time goes in v2:
time: 40.4 us; the launch traced here: 40.2 us
  Pallas kernels  40.2 us (100%)
    pallas_call x1, Pallas kernels, per_device(): pl.pallas_call(functools.partial(slopes_kernel, n, relays, chunks, per, f...  38.3 us
    pallas_call x1, Pallas kernels, per_device(): pl.pallas_call(apply_kernel, out_shape=jax.ShapeDtypeStruct((acts, 2, n *...  1.92 us

profile of v2, /device:TPU:0, one launch (start us, length us, event | category | flops | bytes accessed | tf_op | source)
XLA Modules:
  0.0 40.2 jit_solution(18317256273951807705)
XLA Ops:
  0.0 38.3 %slopes.1.held = bf16[2,512,128]{2,1,0:T(8,128)(2,1)} custom-call(s32[72,128]{1,0:T(8,128)} %bitcast.9, f32[1,72]{1,0:T(1,128)} %bitcast.13, bf16[3,72,8192]{2,1,0:T(8,128)(2,1)} %infl_ref.1, f32[256,32]{1,0:T(8,128)} %bitcast.11, f32[256,32]{1,0:T(8,128)} %bitcast.12, s32[1,32]{1,0:T(1,128)} %bitcast.15, bf16[512,512]{1,0:T(8,128)(2,1)} %constant.2.clone.table_hbm), custom_call_target="tpu_custom_call" | custom-call | tf_op jit(solution)/shard_map/slopes/pallas_call | solution.py:433
  38.3 1.9 %apply.1 = f32[72,2,512]{2,1,0:T(2,128)} custom-call(bf16[2,512,128]{2,1,0:T(8,128)(2,1)} %slopes.1.held, s32[72,128]{1,0:T(8,128)} %bitcast.10, f32[1,72]{1,0:T(1,128)} %bitcast.14), custom_call_target="tpu_custom_call" | custom-call | tf_op jit(solution)/shard_map/apply/pallas_call | solution.py:473

commit v3 on v2

--- a/solution.py
+++ b/solution.py
@@ -10,10 +10,12 @@
 from jax.sharding import PartitionSpec as P
 
 PIX = 16
+CHIP = 4
 NEAR = 4
 FAR = 6
+ASIDE = 6
 AHEAD = 3
-BIAS = 8
+LATER = 3
 MESH = pl.DeviceIdType.MESH
 NT = (((1,), (1,)), ((), ()))
 
@@ -22,7 +24,7 @@
     freqs = np.arange(pixels) - pixels / 2.0
     wave = np.exp(-2j * np.pi * freqs[:, None] * np.arange(samples)[None, :] / (2.0 * samples))
     kron = np.kron(wave, wave)
-    return np.block([[kron.real, -kron.imag], [kron.imag, kron.real]]).astype(np.float32)
+    return np.stack([kron.real, kron.imag]).astype(np.float32)
 
 
 def poly_fit(func, degree):
@@ -66,13 +68,9 @@
     return [jnp.sum(x, axis=0, keepdims=True) for x in (run, along_u, along_v)]
 
 
-def spot_rows(phase, real, imag, table):
-    patterns = phase.shape[0]
-    cs, sn = cos_sin(phase)
-    even = jnp.concatenate([(cs * real).astype(jnp.bfloat16), (cs * imag).astype(jnp.bfloat16)], axis=1)
-    odd = jnp.concatenate([(sn * -imag).astype(jnp.bfloat16), (sn * real).astype(jnp.bfloat16)], axis=1)
-    field = jnp.concatenate([even, odd], axis=0)
-    focal = lax.dot_general(table, field, NT, preferred_element_type=jnp.float32)
+def spot_rows(transform, field):
+    patterns = field.shape[0] // 2
+    focal = lax.dot_general(transform, field, NT, preferred_element_type=jnp.float32)
     half = focal.shape[0] // 2
     squares, crosses = [], []
     for u in range(PIX):
@@ -81,7 +79,7 @@
         c_re, s_re = re[:, :patterns], re[:, patterns:]
         c_im, s_im = im[:, :patterns], im[:, patterns:]
         squares.append((c_re * c_re + c_im * c_im) + (s_re * s_re + s_im * s_im))
-        crosses.append(c_re * s_re + c_im * s_im)
+        crosses.append(c_im * s_re - c_re * s_im)
     p0, pu, pv = column_sums(squares)
     q0, qu, qv = [2.0 * x for x in column_sums(crosses)]
     scale = 1.0 / ((p0 + q0) * (p0 - q0))
@@ -96,23 +94,22 @@
 
 
 def slopes_kernel(
-    n, relays, chunks, per, flat, parts,
+    n, relays, chunks, per, flat, pieces,
     had_hbm, stroke_hbm, infl_ref, amp_hbm, abe_hbm, mask_hbm, table_hbm,
     held_ref,
     had, stroke, amp, abe, mask, table,
-    mid_buf, low_buf, up_buf, cmds, cmds_low, cmds_up, real, imag, rows, mask_rows, mine, passing,
-    load_sems, mid_sems, send_sems, recv_sems, cmd_send, cmd_recv, own_sems, push_send, push_recv, known, pass_send, pass_recv,
+    slabs, cmds, cmds_all, real, imag, transforms, fields, rows, mask_rows, mine, passing,
+    load_sems, mid_sems, send_sems, recv_sems, cmd_send, cmd_recv, own_sems, push_send, push_recv, known, pass_send, pass_recv, forward_send,
 ):
     me = lax.axis_index("tile")
     has_low, has_up = me > 0, me < n - 1
     low_id, up_id = {"tile": jnp.maximum(me - 1, 0)}, {"tile": jnp.minimum(me + 1, n - 1)}
     width = per * flat
-    part = mine.shape[2]
-    subs = parts * part
-    steps = chunks // parts
+    acts = cmds.shape[0]
+    groups, quad = mine.shape[0], mine.shape[1] // 2
+    subs = groups * quad
+    steps = quad // per
     rounds = (n - 1).bit_length()
-    span_up = jnp.where(lax.rem(me, 4) == 3, FAR, NEAR)
-    span_low = jnp.where(lax.rem(me, 4) == 0, FAR, NEAR)
     barrier = pltpu.get_barrier_semaphore()
 
     def greet(sem, distance):
@@ -138,6 +135,7 @@
 
     place = lax.rem(me, 4)
     levels = n // 4
+    mirror = me + 2 - lax.rem(me, 4) // 2 * 4
     far_up = jnp.logical_and(place == 3, has_up)
     far_low = jnp.logical_and(place == 0, has_low)
     pass_up = jnp.logical_and(place == 1, me + 3 < n)
@@ -158,23 +156,21 @@
         return pl.ds(pl.multiple_of(c * width, width), width)
 
     def mid_copy(c):
-        return pltpu.make_async_copy(infl_ref.at[1, :, columns(c)], mid_buf.at[c], mid_sems.at[c])
+        return pltpu.make_async_copy(infl_ref.at[1, :, columns(c)], slabs.at[c, 1, :acts, :], mid_sems.at[c])
 
     def remote(src, dst, send, recv, device):
         return pltpu.make_async_remote_copy(
             src_ref=src, dst_ref=dst, send_sem=send, recv_sem=recv, device_id=device, device_id_type=MESH
         )
 
-    def detour(level, c, count_up):
-        low = chunks * (level + 1) // levels - chunks // BIAS
-        count = chunks - low if count_up else low
+    def picked(c, count):
         return ((c + 1) * count) // chunks != (c * count) // chunks
 
     def via_up(t, c):
-        return detour(t // 4, c, True)
+        return picked(c, chunks * (levels - t // 4 - 1) // levels + chunks // 8)
 
     def via_low(t, c):
-        return detour(t // 4 - 1, c, False)
+        return picked(c, chunks * (t // 4) // levels)
 
     def aside_up(c):
         source = infl_ref.at[2, :, columns(c)]
@@ -186,11 +182,11 @@
 
     def onward_up(c):
         target = {"tile": jnp.minimum(me + 3, n - 1)}
-        return remote(passing.at[c], low_buf.at[c], pass_send.at[c], recv_sems.at[0, c], target)
+        return remote(passing.at[c], slabs.at[c, 0, :acts, :], pass_send.at[c], recv_sems.at[0, c], target)
 
     def onward_low(c):
         target = {"tile": jnp.maximum(me - 3, 0)}
-        return remote(passing.at[c], up_buf.at[c], pass_send.at[c], recv_sems.at[1, c], target)
+        return remote(passing.at[c], slabs.at[c, 2, :acts, :], pass_send.at[c], recv_sems.at[1, c], target)
 
     def relay(c):
         @pl.when(jnp.logical_and(pass_up, via_up(me + 2, c)))
@@ -213,16 +209,16 @@
             onward_low(c).wait_send()
 
     def to_up(c):
-        return remote(infl_ref.at[2, :, columns(c)], low_buf.at[c], send_sems.at[0, c], recv_sems.at[0, c], up_id)
+        return remote(infl_ref.at[2, :, columns(c)], slabs.at[c, 0, :acts, :], send_sems.at[0, c], recv_sems.at[0, c], up_id)
 
     def to_low(c):
-        return remote(infl_ref.at[0, :, columns(c)], up_buf.at[c], send_sems.at[1, c], recv_sems.at[1, c], low_id)
+        return remote(infl_ref.at[0, :, columns(c)], slabs.at[c, 2, :acts, :], send_sems.at[1, c], recv_sems.at[1, c], low_id)
 
     def cmds_to_up():
-        return remote(cmds, cmds_low, cmd_send.at[0], cmd_recv.at[0], up_id)
+        return remote(cmds, cmds_all.at[0, :acts, :], cmd_send.at[0], cmd_recv.at[0], up_id)
 
     def cmds_to_low():
-        return remote(cmds, cmds_up, cmd_send.at[1], cmd_recv.at[1], low_id)
+        return remote(cmds, cmds_all.at[2, :acts, :], cmd_send.at[1], cmd_recv.at[1], low_id)
 
     loads = [
         pltpu.make_async_copy(src, dst, load_sems.at[k])
@@ -239,25 +235,25 @@
             peers += 2 * condition.astype(jnp.int32)
     pl.semaphore_wait(barrier, peers)
 
-    def send_to(exists, far, span, c, straight, aside, via):
-        m = c + span
-        go = jnp.logical_and(exists, jnp.logical_and(m >= 0, m < chunks))
-        around = jnp.logical_and(far, via(me, m)) if relays else False
-
-        @pl.when(jnp.logical_and(go, jnp.logical_not(around)))
-        def _():
-            straight(m).start()
-
+    def send_to(exists, chip, far, c, straight, aside, via):
+        def when(condition, m, copy):
+            @pl.when(jnp.logical_and(condition, jnp.logical_and(m >= 0, m < chunks)))
+            def _():
+                copy(m).start()
+
+        when(chip, c + CHIP, straight)
+        when(jnp.logical_and(exists, jnp.logical_not(jnp.logical_or(chip, far))), c + NEAR, straight)
         if relays:
-            @pl.when(jnp.logical_and(go, around))
-            def _():
-                aside(m).start()
+            when(jnp.logical_and(far, jnp.logical_not(via(me, c + FAR))), c + FAR, straight)
+            when(jnp.logical_and(far, via(me, c + ASIDE)), c + ASIDE, aside)
+        else:
+            when(far, c + FAR, straight)
 
     def send_slab(c):
-        send_to(has_up, far_up, span_up, c, to_up, aside_up, via_up)
-        send_to(has_low, far_low, span_low, c, to_low, aside_low, via_low)
-
-    first = -max(NEAR, FAR)
+        send_to(has_up, lax.rem(me, 2) == 0, far_up, c, to_up, aside_up, via_up)
+        send_to(has_low, lax.rem(me, 2) == 1, far_low, c, to_low, aside_low, via_low)
+
+    first = -max(CHIP, NEAR, FAR, ASIDE)
 
     @pl.loop(first, first + 2)
     def _(c):
@@ -284,26 +280,39 @@
     def _(c):
         mid_copy(c).start()
 
-    @pl.when(jnp.logical_not(has_low))
-    def _():
-        cmds_low[...] = jnp.zeros_like(cmds_low)
-        low_buf[...] = jnp.zeros_like(low_buf)
-
-    @pl.when(jnp.logical_not(has_up))
-    def _():
-        cmds_up[...] = jnp.zeros_like(cmds_up)
-        up_buf[...] = jnp.zeros_like(up_buf)
+    pad = slabs.shape[2] - acts
+    cmds_all[1, :acts] = cmds[...]
+    for o in range(3):
+        if pad:
+            cmds_all[o, acts:] = jnp.zeros((pad, cmds_all.shape[2]), jnp.bfloat16)
+            slabs[:, o, acts:] = jnp.zeros((chunks, pad, width), jnp.bfloat16)
+
+    for absent, o in ((jnp.logical_not(has_low), 0), (jnp.logical_not(has_up), 2)):
+        @pl.when(absent)
+        def _():
+            cmds_all[o] = jnp.zeros(cmds_all.shape[1:], jnp.bfloat16)
+
+            @pl.loop(0, chunks)
+            def _(c):
+                slabs[c, o] = jnp.zeros(slabs.shape[2:], jnp.bfloat16)
 
     for load in loads[2:]:
         load.wait()
     cs, sn = cos_sin(abe[...])
-    whole_real, whole_imag = (amp[...] * cs).T, (amp[...] * sn).T
-    for c in range(chunks):
-        real[c] = whole_real[c * per:(c + 1) * per]
-        imag[c] = whole_imag[c * per:(c + 1) * per]
+    real[...] = (amp[...] * cs).T.reshape(real.shape)
+    imag[...] = (amp[...] * sn).T.reshape(imag.shape)
+
+    @pl.loop(0, subs)
+    def _(k):
+        re, im = real[k], imag[k]
+        half = table.shape[1]
+        transforms[k, :half] = (table[0] * re - table[1] * im).astype(jnp.bfloat16)
+        transforms[k, half:] = (table[0] * im + table[1] * re).astype(jnp.bfloat16)
+
     mask_column = diagonal_column(mask[...].astype(jnp.float32))
-    for g in range(parts):
-        mask_rows[g] = jnp.broadcast_to(mask_column[g * part:(g + 1) * part], mask_rows.shape[1:])
+    for g in range(groups):
+        column_of = mask_column[g * quad:(g + 1) * quad]
+        mask_rows[g] = jnp.broadcast_to(jnp.concatenate([column_of, column_of], axis=0), mask_rows.shape[1:])
 
     @pl.when(has_up)
     def _():
@@ -320,21 +329,50 @@
         def _(c):
             relay(c)
 
-    mid_cmds = cmds[...].T
-    low_cmds = cmds_low[...].T
-    up_cmds = cmds_up[...].T
-
-    def slot(g):
-        return held_ref.at[:, pl.ds(pl.multiple_of(me * subs + g * part, part), part), :]
-
-    def own(g):
-        return pltpu.make_async_copy(mine.at[g], slot(g), own_sems.at[g])
-
-    def push(g, k):
-        return remote(mine.at[g], slot(g), push_send.at[g, k], push_recv.at[g, k], {"tile": lax.rem(me + k, n)})
-
-    @pl.loop(0, chunks)
-    def _(c):
+    all_cmds = cmds_all[...].reshape(3 * slabs.shape[2], cmds.shape[1]).T
+
+    def slot(p, t):
+        start, size = pieces[p]
+        return held_ref.at[pl.ds(t * groups + start, size)]
+
+    def piece(p):
+        start, size = pieces[p]
+        return mine.at[pl.ds(start, size)]
+
+    def own(p):
+        return pltpu.make_async_copy(piece(p), slot(p, me), own_sems.at[p])
+
+    def push(p, t):
+        return remote(piece(p), slot(p, me), push_send.at[p, t], push_recv.at[p, me], {"tile": t})
+
+    def forward(p, t):
+        return remote(slot(p, mirror), slot(p, mirror), forward_send.at[p, t], push_recv.at[p, mirror], {"tile": t})
+
+    def landing(p, t):
+        return remote(piece(p), slot(p, t), push_send.at[p, t], push_recv.at[p, t], {"tile": t})
+
+    def mirrored(p):
+        return relays and p == 0 and len(pieces) > 2
+
+    def everyone(act):
+        @pl.loop(1, n)
+        def _(k):
+            act(lax.rem(me + k, n))
+
+    def column(act):
+        @pl.loop(1, n // 2)
+        def _(k):
+            at = lax.rem(me // 4 * 2 + lax.rem(me, 2) + k, n // 2)
+            act(at // 2 * 4 + lax.rem(me, 4) // 2 * 2 + lax.rem(at, 2))
+
+    def spread(p, act):
+        if mirrored(p):
+            column(lambda t: act(push(p, t)))
+            act(push(p, mirror))
+        else:
+            everyone(lambda t: act(push(p, t)))
+
+    def arrive(c):
         mid_copy(c).wait()
 
         @pl.when(has_low)
@@ -351,20 +389,26 @@
             def _():
                 relay(c + AHEAD)
 
+    def wavefront(c):
+        for k in range(per):
+            block = slabs[c, :, :, k * flat:(k + 1) * flat].reshape(all_cmds.shape[1], flat)
+            cs, sn = cos_sin(jnp.dot(all_cmds, block, preferred_element_type=jnp.float32))
+            half = cs.shape[0]
+            fields[lax.rem(c, 2), k, :half] = cs.astype(jnp.bfloat16)
+            fields[lax.rem(c, 2), k, half:] = sn.astype(jnp.bfloat16)
+
+    def spots(c):
         rows_u, rows_v = [], []
         for k in range(per):
-            cols = slice(k * flat, (k + 1) * flat)
-            phase = jnp.dot(low_cmds, low_buf[c, :, cols], preferred_element_type=jnp.float32)
-            phase += jnp.dot(mid_cmds, mid_buf[c, :, cols], preferred_element_type=jnp.float32)
-            phase += jnp.dot(up_cmds, up_buf[c, :, cols], preferred_element_type=jnp.float32)
-            along_u, along_v = spot_rows(phase, real[c, k:k + 1, :], imag[c, k:k + 1, :], table[...])
+            along_u, along_v = spot_rows(transforms[c * per + k], fields[lax.rem(c, 2), k])
             rows_u.append(along_u)
             rows_v.append(along_v)
         rows[c, 0] = jnp.concatenate(rows_u, axis=0)
         rows[c, 1] = jnp.concatenate(rows_v, axis=0)
 
+    def finish(c):
         for r in range(rounds):
-            @pl.when(c == r * steps // rounds)
+            @pl.when(c == r)
             def _():
                 met(known.at[r], 2 ** r)
                 if r + 1 < rounds:
@@ -373,14 +417,35 @@
         @pl.when(lax.rem(c, steps) == steps - 1)
         def _():
             g = c // steps
-            for j in range(2):
-                whole = jnp.concatenate([rows[g * steps + i, j] for i in range(steps)], axis=0)
-                mine[g, j] = (whole * mask_rows[g]).astype(mine.dtype)
-            own(g).start()
-
-            @pl.loop(1, n)
-            def _(k):
-                push(g, k).start()
+            both = [rows[g * steps + i, j] for j in range(2) for i in range(steps)]
+            mine[g] = (jnp.concatenate(both, axis=0) * mask_rows[g]).astype(mine.dtype)
+
+        for p, (start, size) in enumerate(pieces):
+            end = (start + size) * steps - 1
+
+            @pl.when(c == end)
+            def _():
+                own(p).start()
+                spread(p, lambda copy: copy.start())
+
+            if mirrored(p):
+                @pl.when(c == end + LATER)
+                def _():
+                    landing(p, mirror).wait_recv()
+                    column(lambda t: forward(p, t).start())
+
+    arrive(0)
+    wavefront(0)
+
+    @pl.loop(1, chunks)
+    def _(c):
+        arrive(c)
+        spots(c - 1)
+        wavefront(c)
+        finish(c - 1)
+
+    spots(chunks - 1)
+    finish(chunks - 1)
 
     @pl.loop(0, chunks)
     def _(c):
@@ -395,21 +460,36 @@
         if relays:
             relay_done(c)
 
-    @pl.loop(0, parts)
-    def _(g):
-        own(g).wait()
-
-        @pl.loop(1, n)
-        def _(k):
-            push(g, k).wait()
+    for p in range(len(pieces)):
+        own(p).wait()
+        spread(p, lambda copy: copy.wait_send())
+        if mirrored(p):
+            column(lambda t: forward(p, t).wait_send())
+
+        def landed(t):
+            if mirrored(p):
+                @pl.when(t != mirror)
+                def _():
+                    landing(p, t).wait_recv()
+            else:
+                landing(p, t).wait_recv()
+
+        everyone(landed)
 
 
 def apply_kernel(held, had_ref, stroke_ref, out_ref):
     patterns = had_ref.shape[1]
+    blocks, height = held.shape[0], held.shape[1]
     signs = had_ref[...].astype(jnp.float32).astype(jnp.bfloat16)
     scale = patterns * diagonal_column(stroke_ref[...])
-    for c in range(2):
-        summed = lax.dot_general(signs, held[c], NT, preferred_element_type=jnp.float32)
+    pairs = held[...].astype(jnp.float32).reshape(blocks // 2, 2, height, patterns)
+    first, second = pairs[:, 0], pairs[:, 1]
+    upper = lax.broadcasted_iota(jnp.int32, first.shape, 1) < height // 2
+    along_u = jnp.where(upper, first, pltpu.roll(second, height // 2, 1))
+    along_v = jnp.where(upper, pltpu.roll(first, height // 2, 1), second)
+    for c, along in enumerate((along_u, along_v)):
+        slopes = along.reshape(blocks * height // 2, patterns).astype(jnp.bfloat16)
+        summed = lax.dot_general(signs, slopes, NT, preferred_element_type=jnp.float32)
         out_ref[:, c, :] = summed / scale
 
 
@@ -420,37 +500,42 @@
     flat = samples * samples
     per = math.gcd(subs, 2)
     chunks = subs // per
-    parts = subs // 8 if subs % 8 == 0 else 1
+    groups = subs // 4
+    bounds = [0, groups - 3, groups - 1, groups] if groups > 4 else [0, groups]
+    pieces = tuple((a, b - a) for a, b in zip(bounds, bounds[1:]))
+    parts = len(pieces)
     had = hadamard.T
     amp = amplitude.transpose(1, 2, 0).reshape(flat, subs)
     abe = aberration.transpose(1, 2, 0).reshape(flat, subs)
     stroke = stroke.reshape(1, acts)
     mask = valid_mask.reshape(1, subs)
-    table = jnp.asarray(dft_table(samples, PIX), dtype=jnp.bfloat16)
+    table = jnp.asarray(dft_table(samples, PIX), dtype=jnp.float32)
+    depth = -(-acts // 16) * 16
     vmem = pl.BlockSpec(memory_space=pltpu.VMEM)
     hbm = pl.BlockSpec(memory_space=pltpu.HBM)
     slab = pltpu.VMEM((chunks, acts, per * flat), jnp.bfloat16)
     held = pl.pallas_call(
-        functools.partial(slopes_kernel, n, relays, chunks, per, flat, parts),
-        out_shape=jax.ShapeDtypeStruct((2, n * subs, patterns), jnp.bfloat16),
+        functools.partial(slopes_kernel, n, relays, chunks, per, flat, pieces),
+        out_shape=jax.ShapeDtypeStruct((n * groups, 8, patterns), jnp.bfloat16),
         in_specs=[hbm] * 7,
-        out_specs=hbm,
+        out_specs=vmem,
         scratch_shapes=[
             pltpu.VMEM((acts, patterns), jnp.int32),
             pltpu.VMEM((1, acts), jnp.float32),
             pltpu.VMEM((flat, subs), jnp.float32),
             pltpu.VMEM((flat, subs), jnp.float32),
             pltpu.VMEM((1, subs), jnp.int32),
-            pltpu.VMEM(table.shape, jnp.bfloat16),
-            slab, slab, slab,
+            pltpu.VMEM(table.shape, jnp.float32),
+            pltpu.VMEM((chunks, 3, depth, per * flat), jnp.bfloat16),
             pltpu.VMEM((acts, patterns), jnp.bfloat16),
-            pltpu.VMEM((acts, patterns), jnp.bfloat16),
-            pltpu.VMEM((acts, patterns), jnp.bfloat16),
-            pltpu.VMEM((chunks, per, flat), jnp.float32),
-            pltpu.VMEM((chunks, per, flat), jnp.float32),
+            pltpu.VMEM((3, depth, patterns), jnp.bfloat16),
+            pltpu.VMEM((subs, 1, flat), jnp.float32),
+            pltpu.VMEM((subs, 1, flat), jnp.float32),
+            pltpu.VMEM((subs, 2 * PIX * PIX, flat), jnp.bfloat16),
+            pltpu.VMEM((2, per, 2 * patterns, flat), jnp.bfloat16),
             pltpu.VMEM((chunks, 2, per, patterns), jnp.float32),
-            pltpu.VMEM((parts, subs // parts, patterns), jnp.float32),
-            pltpu.VMEM((parts, 2, subs // parts, patterns), jnp.bfloat16),
+            pltpu.VMEM((groups, 8, patterns), jnp.float32),
+            pltpu.VMEM((groups, 8, patterns), jnp.bfloat16),
             slab if relays else pltpu.VMEM((8, 128), jnp.bfloat16),
             pltpu.SemaphoreType.DMA((6,)),
             pltpu.SemaphoreType.DMA((chunks,)),
@@ -464,17 +549,19 @@
             pltpu.SemaphoreType.REGULAR(((n - 1).bit_length(),)),
             pltpu.SemaphoreType.DMA((chunks,)),
             pltpu.SemaphoreType.DMA((chunks,)),
+            pltpu.SemaphoreType.DMA((parts, n)),
         ],
         compiler_params=pltpu.CompilerParams(
-            collective_id=1, has_side_effects=True, vmem_limit_bytes=62 * 1024 * 1024
+            collective_id=1, has_side_effects=True, vmem_limit_bytes=40 * 1024 * 1024
         ),
         name="slopes",
-    )(had, stroke, influence, amp, abe, mask, table)
+    )(*(pltpu.with_memory_space_constraint(x, pltpu.HBM) for x in (had, stroke, influence, amp, abe, mask, table)))
     return pl.pallas_call(
         apply_kernel,
         out_shape=jax.ShapeDtypeStruct((acts, 2, n * subs), jnp.float32),
         in_specs=[vmem] * 3,
         out_specs=vmem,
+        compiler_params=pltpu.CompilerParams(vmem_limit_bytes=24 * 1024 * 1024),
         name="apply",
     )(held, had, stroke)
 

time: 40.4 us -> 38.5 us (0.953)
  Pallas kernels: 40.2 us -> 38.3 us
    pallas_call x1, Pallas kernels: 38.3 us -> 37.3 us  [per_device(): pl.pallas_call(functools.partial(slopes_kernel, n, relays, chunks, per, f...]
    pallas_call x1, Pallas kernels: 1.92 us -> 0.97 us  [per_device(): pl.pallas_call(apply_kernel, out_shape=jax.ShapeDtypeStruct((acts, 2, n *...]
where the time goes in v3:
time: 38.5 us; the launch traced here: 38.3 us
  Pallas kernels  38.3 us (99%)
    pallas_call x1, Pallas kernels, per_device(): pl.pallas_call(functools.partial(slopes_kernel, n, relays, chunks, per, f...  37.3 us
    pallas_call x1, Pallas kernels, per_device(): pl.pallas_call(apply_kernel, out_shape=jax.ShapeDtypeStruct((acts, 2, n *...  0.97 us

profile of v3, /device:TPU:0, one launch (start us, length us, event | category | flops | bytes accessed | tf_op | source)
XLA Modules:
  0.0 38.3 jit_solution(11484134732599102795)
XLA Ops:
  0.0 0.0 copy-start.1
  0.0 0.0 copy-start
  0.0 37.3 %slopes.1.held = bf16[128,8,128]{2,1,0:T(8,128)(2,1)S(1)} custom-call(s32[72,128]{1,0:T(8,128)} %bitcast.9, f32[1,72]{1,0:T(1,128)} %bitcast.11, bf16[3,72,8192]{2,1,0:T(8,128)(2,1)} %infl_ref.1, f32[256,32]{1,0:T(8,128)} %bitcast.13, f32[256,32]{1,0:T(8,128)} %bitcast.14, s32[1,32]{1,0:T(1,128)} %bitcast.15, f32[2,256,256]{2,1,0:T(8,128)} %constant.2.clone.table_hbm), custom_call_target="tpu_custom_call" | custom-call | tf_op jit(solution)/shard_map/slopes/pallas_call | solution.py:517
  37.3 0.0 copy-done.1
  37.3 0.0 copy-done
  37.3 1.0 %apply.1 = f32[72,2,512]{2,1,0:T(2,128)} custom-call(bf16[128,8,128]{2,1,0:T(8,128)(2,1)S(1)} %slopes.1.held, s32[72,128]{1,0:T(8,128)S(1)} %bitcast.10, f32[1,72]{1,0:T(1,128)S(1)} %bitcast.12), custom_call_target="tpu_custom_call" | custom-call | tf_op jit(solution)/shard_map/apply/pallas_call | solution.py:559
Async XLA Ops:
  0.0 37.3 %copy-start.1 = (f32[72]{0:T(128)S(1)}, f32[72]{0:T(128)}, u32[]{:S(2)}) copy-start(f32[72]{0:T(128)} %param.8) | copy-start | bytes 868
  0.0 37.3 %copy-start = (s32[128,72]{0,1:T(8,128)S(1)}, s32[128,72]{0,1:T(8,128)}, u32[]{:S(2)}) copy-start(s32[128,72]{0,1:T(8,128)} %param.7) | copy-start | bytes 110596
